TPU v7x, 32 devices: a whole 2x2x4 slice. The times are simulated.
32 devices in a mesh: gx: 2 (over y), gy: 4 (over z), gz: 4 (over x, core).
Axes of the slice: x: 2, y: 2, z: 4, core: 2. Of those that a mesh axis runs over, the one named last changes fastest.
Arguments:
- tokens: bfloat16 [512, 6144], P(('gx', 'gy'), 'gz'), may hold values from -6 to 6
- grad_out: bfloat16 [512, 6144], P(('gx', 'gy'), 'gz'), may hold values from -1.5 to 1.5
- w_in: bfloat16 [6144, 12288], P('gz', ('gy', 'gx')), may hold values from -0.078125 to 0.078125
- w_out: bfloat16 [12288, 6144], P(('gy', 'gx'), 'gz'), may hold values from -0.0546875 to 0.0546875
Outputs:
- mlp_out: bfloat16 [512, 6144], P(('gx', 'gy'), 'gz')
- tok_grad: bfloat16 [512, 6144], P(('gx', 'gy'), 'gz')
- win_grad: float32 [6144, 12288], P('gz', ('gy', 'gx'))
- wout_grad: float32 [12288, 6144], P(('gy', 'gx'), 'gz')
All inputs are finite; a program needn't handle non-finite values.
Results may differ from a plain program's by a relative error of at most 0.01.
Values may be sent and summed in bfloat16 or wider, within the bound.
A program may use at most 128 MiB of HBM per device.

v0:
```python
import math
import jax
import jax.numpy as jnp
from jax import lax
from jax.sharding import PartitionSpec as P


def gelu_slope(values):
    cdf = 0.5 * (1.0 + jax.scipy.special.erf(values * 0.7071067811865476))
    density = jnp.exp(-0.5 * values * values) * 0.3989422804014327
    return cdf + values * density


def contract_last(left, right):
    return lax.dot_general(
        left, right, (((1,), (1,)), ((), ())), preferred_element_type=jnp.float32
    )


def contract_first(left, right):
    return lax.dot_general(
        left, right, (((0,), (0,)), ((), ())), preferred_element_type=jnp.float32
    )


def per_device(tokens, grad_out, w_in, w_out):
    tok_rows, grad_rows = (
        lax.all_gather(tokens, "gy", axis=0, tiled=True),
        lax.all_gather(grad_out, "gy", axis=0, tiled=True),
    )
    win_tile, wout_tile = (
        lax.all_gather(w_in, "gx", axis=1, tiled=True),
        lax.all_gather(w_out, "gx", axis=0, tiled=True),
    )
    row_total = tok_rows.shape[0]
    block_scale = 1.0 / math.sqrt(row_total)
    pre_part = lax.psum_scatter(
        jnp.dot(tok_rows, win_tile, preferred_element_type=jnp.float32),
        "gz",
        scatter_dimension=0,
        tiled=True,
    )
    act_part = jax.nn.gelu(pre_part, approximate=False).astype(jnp.bfloat16)
    act_all = lax.all_gather(act_part, "gz", axis=0, tiled=True)
    mlp_out = lax.psum_scatter(
        jnp.dot(act_all, wout_tile, preferred_element_type=jnp.float32),
        "gy",
        scatter_dimension=0,
        tiled=True,
    ).astype(jnp.bfloat16)
    wout_grad = lax.psum_scatter(
        (contract_first(act_all, grad_rows) * block_scale).astype(jnp.bfloat16),
        "gx",
        scatter_dimension=0,
        tiled=True,
    ).astype(jnp.float32)
    dact_part = lax.psum_scatter(
        contract_last(grad_rows, wout_tile), "gz", scatter_dimension=0, tiled=True
    )
    dpre_part = (dact_part * gelu_slope(pre_part)).astype(jnp.bfloat16)
    dpre_all = lax.all_gather(dpre_part, "gz", axis=0, tiled=True)
    tok_grad = lax.psum_scatter(
        contract_last(dpre_all, win_tile), "gy", scatter_dimension=0, tiled=True
    ).astype(jnp.bfloat16)
    win_term = contract_first(tok_rows, dpre_all) * block_scale
    win_grad = lax.psum_scatter(
        win_term.astype(jnp.bfloat16), "gx", scatter_dimension=1, tiled=True
    ).astype(jnp.float32)
    return (mlp_out, tok_grad, win_grad, wout_grad)


def solution(mesh):
    in_specs = (
        P(("gx", "gy"), "gz"),
        P(("gx", "gy"), "gz"),
        P("gz", ("gy", "gx")),
        P(("gy", "gx"), "gz"),
    )
    out_specs = (
        P(("gx", "gy"), "gz"),
        P(("gx", "gy"), "gz"),
        P("gz", ("gy", "gx")),
        P(("gy", "gx"), "gz"),
    )
    return jax.shard_map(
        per_device, mesh=mesh, in_specs=in_specs, out_specs=out_specs, check_vma=False
    )
```

profile of v0, /device:TPU:0, one launch (start us, length us, event | category | flops | bytes accessed | tf_op | source)
XLA Modules:
  0.0 691.5 jit_solution(6097030964073734867)
XLA Ops:
  7.2 0.7 all-gather.9.cloned.1.call-update
  8.0 0.7 all-gather.5.cloned.1.call-update
  8.7 21.3 %all_gather.22 = bf16[256,1536]{1,0:T(8,128)(2,1)S(1)} all-gather(bf16[64,1536]{1,0:T(8,128)(2,1)S(1)} %copy-done), channel_id=1, replica_groups=mesh['gx'=2,'gy'=4,'gz'=4] {'gy'}, dimensions={0}, use_global_device_ids=true | all-gather | bytes 983040 | tf_op jit(solution)/shard_map/all_gather | solution.py:29
  30.0 100.3 %all-gather.9.cloned.1.call-done = bf16[3072,1536]{1,0:T(8,128)(2,1)} async-done(((bf16[1536,1536]{1,0:T(8,128)(2,1)}), bf16[3072,1536]{1,0:T(8,128)(2,1)}) %all-gather.9.cloned.1.call-update) | async-done | bytes 9437200 | tf_op jit(solution)/shard_map/all_gather | solution.py:33
  130.3 8.0 %fusion.19 = f32[256,3072]{1,0:T(8,128)} fusion(bf16[256,1536]{1,0:T(8,128)(2,1)S(1)} %all_gather.22, bf16[3072,1536]{1,0:T(8,128)(2,1)} %all-gather.9.cloned.1.call-done), kind=kOutput, calls=%fused_computation.31 | convolution fusion | flops 2415919104 | bytes 13369344 | tf_op jit(solution)/shard_map/dot_general | solution.py:15
  138.3 0.0 reduce-scatter.7.cloned.1.call-start
  138.3 19.6 %all_gather.18 = bf16[256,1536]{1,0:T(8,128)(2,1)S(1)} all-gather(bf16[64,1536]{1,0:T(8,128)(2,1)S(1)} %copy-done.1), channel_id=1, replica_groups=mesh['gx'=2,'gy'=4,'gz'=4] {'gy'}, dimensions={0}, use_global_device_ids=true | all-gather | bytes 983040 | tf_op jit(solution)/shard_map/all_gather | solution.py:28
  157.9 91.9 %all-gather.5.cloned.1.call-done = bf16[1536,3072]{1,0:T(8,128)(2,1)} async-done(((bf16[1536,1536]{1,0:T(8,128)(2,1)}), bf16[1536,3072]{1,0:T(8,128)(2,1)}) %all-gather.5.cloned.1.call-update) | async-done | bytes 9437200 | tf_op jit(solution)/shard_map/all_gather | solution.py:32
  249.8 7.9 %fusion.17 = f32[256,3072]{1,0:T(8,128)} fusion(bf16[256,1536]{1,0:T(8,128)(2,1)S(1)} %all_gather.18, bf16[1536,3072]{1,0:T(8,128)(2,1)} %all-gather.5.cloned.1.call-done), kind=kOutput, calls=%fused_computation.29 | convolution fusion | flops 2415919104 | bytes 13369344 | tf_op jit(solution)/shard_map/dot_general | solution.py:38
  257.8 0.0 all-gather.11.cloned.1.call-start
  257.9 33.0 %reduce-scatter.11.cloned.1.call-done = f32[64,3072]{1,0:T(8,128)} async-done(((f32[256,3072]{1,0:T(8,128)}), f32[64,3072]{1,0:T(8,128)}) %reduce-scatter.11.cloned.1.call-update) | async-done | bytes 786448 | tf_op jit(solution)/shard_map/reduce_scatter | solution.py:57
  290.9 40.9 %reduce-scatter.7.cloned.1.call-done = f32[64,3072]{1,0:T(8,128)} async-done(((f32[256,3072]{1,0:T(8,128)}), f32[64,3072]{1,0:T(8,128)}) %reduce-scatter.7.cloned.1.call-update) | async-done | bytes 786448 | tf_op jit(solution)/shard_map/reduce_scatter | solution.py:37
  331.7 3.8 fusion.9
  335.6 0.0 all-gather.7.cloned.1.call-start
  335.6 0.5 all-gather.7.cloned.1.call-update
  336.2 19.2 %all-gather.11.cloned.1.call-done = bf16[256,3072]{1,0:T(8,128)(2,1)} async-done(((bf16[64,3072]{1,0:T(8,128)(2,1)}), bf16[256,3072]{1,0:T(8,128)(2,1)}) %all-gather.11.cloned.1.call-update) | async-done | bytes 1572880 | tf_op jit(solution)/shard_map/all_gather | solution.py:61
  355.4 8.0 %fusion.20 = f32[256,1536]{1,0:T(8,128)} fusion(bf16[256,3072]{1,0:T(8,128)(2,1)} %all-gather.11.cloned.1.call-done, bf16[1536,3072]{1,0:T(8,128)(2,1)} %all-gather.5.cloned.1.call-done), kind=kOutput, calls=%fused_computation.32 | convolution fusion | flops 2415919104 | bytes 12582912 | tf_op jit(solution)/shard_map/dot_general | solution.py:15
  363.4 0.0 reduce-scatter.9.cloned.1.call-start
  363.4 13.6 %all-gather.7.cloned.1.call-done = bf16[256,3072]{1,0:T(8,128)(2,1)} async-done(((bf16[64,3072]{1,0:T(8,128)(2,1)}), bf16[256,3072]{1,0:T(8,128)(2,1)}) %all-gather.7.cloned.1.call-update) | async-done | bytes 1572880 | tf_op jit(solution)/shard_map/all_gather | solution.py:44
  377.0 7.9 %fusion.18 = f32[256,1536]{1,0:T(8,128)} fusion(bf16[256,3072]{1,0:T(8,128)(2,1)} %all-gather.7.cloned.1.call-done, bf16[3072,1536]{1,0:T(8,128)(2,1)} %all-gather.9.cloned.1.call-done), kind=kOutput, calls=%fused_computation.30 | convolution fusion | flops 2415919104 | bytes 12582912 | tf_op jit(solution)/shard_map/dot_general | solution.py:46
  385.0 0.0 reduce-scatter.17.cloned.1.call-start
  385.0 6.8 multiply_convert_fusion
  391.8 0.2 reduce-scatter.15.cloned.1.call-start
  392.0 5.2 fusion
  397.3 17.5 %reduce-scatter.13.cloned.1.call-done = f32[64,1536]{1,0:T(8,128)} async-done(((f32[256,1536]{1,0:T(8,128)}), f32[64,1536]{1,0:T(8,128)}) %reduce-scatter.13.cloned.1.call-update) | async-done | bytes 393232 | tf_op jit(solution)/shard_map/reduce_scatter | solution.py:62
  414.8 1.7 convert_element_type.30
  416.5 34.9 %reduce-scatter.9.cloned.1.call-done = f32[64,1536]{1,0:T(8,128)} async-done(((f32[256,1536]{1,0:T(8,128)}), f32[64,1536]{1,0:T(8,128)}) %reduce-scatter.9.cloned.1.call-update) | async-done | bytes 393232 | tf_op jit(solution)/shard_map/reduce_scatter | solution.py:45
  451.4 1.7 convert_element_type.28
  453.1 110.7 %reduce-scatter.17.cloned.1.call-done = bf16[1536,1536]{1,0:T(8,128)(2,1)} async-done(((bf16[3072,1536]{1,0:T(8,128)(2,1)}), bf16[1536,1536]{1,0:T(8,128)(2,1)}) %reduce-scatter.17.cloned.1.call-update) | async-done | bytes 4718608 | tf_op jit(solution)/shard_map/reduce_scatter | solution.py:51
  563.8 7.4 %convert_element_type.35 = f32[1536,1536]{1,0:T(8,128)} convert(bf16[1536,1536]{1,0:T(8,128)(2,1)} %reduce-scatter.17.cloned.1.call-done) | non-fusion elementwise | flops 2359296 | bytes 14155776 | tf_op jit(solution)/shard_map/convert_element_type | solution.py:56
  571.2 106.0 %reduce-scatter.15.cloned.1.call-done = bf16[1536,1536]{0,1:T(8,128)(2,1)} async-done(((bf16[1536,3072]{0,1:T(8,128)(2,1)}), bf16[1536,1536]{0,1:T(8,128)(2,1)}) %reduce-scatter.15.cloned.1.call-update) | async-done | bytes 4718608 | tf_op jit(solution)/shard_map/reduce_scatter | solution.py:66
  677.2 7.4 %copy.8 = f32[1536,1536]{1,0:T(8,128)} copy(bf16[1536,1536]{0,1:T(8,128)(2,1)} %reduce-scatter.15.cloned.1.call-done) | data formatting | bytes 14155776
  (17 shorter events, 0.3 us)
Async XLA Ops:
  7.2 1.5 copy-start
  7.2 123.1 %all-gather.9.cloned.1.call-start = ((), (), s32[]{:S(2)}) async-start(), calls=%async_computation.9 | async-start | bytes 14155776 | tf_op jit(solution)/shard_map/all_gather | solution.py:33
  7.9 241.9 %all-gather.5.cloned.1.call-start = ((), (), s32[]{:S(2)}) async-start(), calls=%async_computation.6 | async-start | bytes 14155776 | tf_op jit(solution)/shard_map/all_gather | solution.py:32
  8.7 282.2 %reduce-scatter.11.cloned.1.call-start = ((), (), s32[]{:S(2)}) async-start(), calls=%async_computation.11 | async-start | bytes 3932160 | tf_op jit(solution)/shard_map/reduce_scatter | solution.py:57
  30.0 108.3 %copy-start.1 = (bf16[64,1536]{1,0:T(8,128)(2,1)S(1)}, bf16[64,1536]{1,0:T(8,128)(2,1)}, u32[]{:S(2)}) copy-start(bf16[64,1536]{1,0:T(8,128)(2,1)} %param.4) | copy-start | bytes 589828
  138.3 193.4 %reduce-scatter.7.cloned.1.call-start = ((), (), s32[]{:S(2)}) async-start(), calls=%async_computation.7 | async-start | bytes 3932160 | tf_op jit(solution)/shard_map/reduce_scatter | solution.py:37
  257.8 97.6 %all-gather.11.cloned.1.call-start = ((), (), s32[]{:S(2)}) async-start(), calls=%async_computation.12 | async-start | bytes 1966080 | tf_op jit(solution)/shard_map/all_gather | solution.py:61
  335.6 41.5 %all-gather.7.cloned.1.call-start = ((), (), s32[]{:S(2)}) async-start(), calls=%async_computation.8 | async-start | bytes 1966080 | tf_op jit(solution)/shard_map/all_gather | solution.py:44
  336.2 78.6 %reduce-scatter.13.cloned.1.call-start = ((), (), s32[]{:S(2)}) async-start(), calls=%async_computation.13 | async-start | bytes 1966080 | tf_op jit(solution)/shard_map/reduce_scatter | solution.py:62
  363.4 88.1 %reduce-scatter.9.cloned.1.call-start = ((), (), s32[]{:S(2)}) async-start(), calls=%async_computation.10 | async-start | bytes 1966080 | tf_op jit(solution)/shard_map/reduce_scatter | solution.py:45
  385.0 7.1 %copy-start.2 = (bf16[256,3072]{1,0:T(8,128)(2,1)S(1)}, bf16[256,3072]{1,0:T(8,128)(2,1)}, u32[]{:S(2)}) copy-start(bf16[256,3072]{1,0:T(8,128)(2,1)} %all-gather.11.cloned.1.call-done) | copy-start | bytes 4718596
  385.0 178.8 %reduce-scatter.17.cloned.1.call-start = ((), (), s32[]{:S(2)}) async-start(), calls=%async_computation.15 | async-start | bytes 14155776 | tf_op jit(solution)/shard_map/reduce_scatter | solution.py:51
  391.8 285.4 %reduce-scatter.15.cloned.1.call-start = ((), (), s32[]{:S(2)}) async-start(), calls=%async_computation.14 | async-start | bytes 14155776 | tf_op jit(solution)/shard_map/reduce_scatter | solution.py:66
Sparse Core Ops, SparseCore 0:
  9.5 120.6 all-gather.8
  131.8 117.9 all-gather.4
  252.9 37.8 reduce-scatter.10
  293.8 37.8 reduce-scatter.6
  335.7 19.6 all-gather.10
  357.4 19.6 all-gather.6
  379.3 35.4 reduce-scatter.12
  417.1 34.2 reduce-scatter.8
  454.3 109.4 reduce-scatter.16
  566.5 110.6 reduce-scatter.14
where the time goes:
time: 692 us; the launch traced here: 691 us
  waiting for transfers between devices  570 us (82%)
  matrix products  43.7 us (6%)
  blocking collectives  40.9 us (6%)
  other arithmetic  14.6 us (2%)
  between operations  14.2 us (2%)
  local copies, waits for them, and re-layouts  7.41 us (1%)
    reduce_scatter x1, waiting for transfers between devices, per_device(): lax.psum_scatter((contract_first(act_all, grad_rows) * block_scale).astyp...  111 us
    reduce_scatter x1, waiting for transfers between devices, per_device(): lax.psum_scatter(win_term.astype(jnp.bfloat16), 'gx', scatter_dimension=1...  106 us
    all_gather x1, waiting for transfers between devices, per_device(): lax.all_gather(w_out, 'gx', axis=0, tiled=True)  100 us
    all_gather x1, waiting for transfers between devices, per_device(): lax.all_gather(w_in, 'gx', axis=1, tiled=True)  91.9 us
    reduce_scatter x1, waiting for transfers between devices, per_device(): lax.psum_scatter(jnp.dot(tok_rows, win_tile, preferred_element_type=jnp.f...  40.9 us
    reduce_scatter x1, waiting for transfers between devices, per_device(): lax.psum_scatter(jnp.dot(act_all, wout_tile, preferred_element_type=jnp.f...  34.9 us
    reduce_scatter x1, waiting for transfers between devices, per_device(): lax.psum_scatter(contract_last(grad_rows, wout_tile), 'gz', scatter_dimen...  33 us
    all_gather x1, blocking collectives, per_device(): lax.all_gather(grad_out, 'gy', axis=0, tiled=True)  21.3 us
  transfers between devices with their start and end apart: 10, of which 10 were waited for; matrix products, arithmetic and copies ran while one was open for 8% of the time, Pallas kernels for 0%

commit v1 on v0

--- a/solution.py
+++ b/solution.py
@@ -29,7 +29,9 @@
         lax.all_gather(grad_out, "gy", axis=0, tiled=True),
     )
     win_tile, wout_tile = (
-        lax.all_gather(w_in, "gx", axis=1, tiled=True),
+        jnp.concatenate(
+            lax.all_to_all(jnp.stack([w_in] * lax.axis_size("gx")), "gx", 0, 0), axis=1
+        ),
         lax.all_gather(w_out, "gx", axis=0, tiled=True),
     )
     row_total = tok_rows.shape[0]

time: 692 us -> 663 us (0.958)
  waiting for transfers between devices: 570 us -> 514 us
  other arithmetic: 14.6 us -> 24.5 us
  local copies, waits for them, and re-layouts: 7.41 us -> 16.4 us
  starting transfers between devices: 0.58 us -> 8.53 us
    all_to_all x0 -> x1, waiting for transfers between devices: none -> 177 us  [per_device(): lax.all_to_all(jnp.stack([w_in] * lax.axis_size('gx')), 'gx', 0, 0)]
    all_gather x1, waiting for transfers between devices: 100 us -> 0.01 us  [per_device(): lax.all_gather(w_out, 'gx', axis=0, tiled=True)]
    all_gather x1 -> x0, waiting for transfers between devices: 91.9 us -> none  [per_device(): lax.all_gather(w_in, 'gx', axis=1, tiled=True)]
    reduce_scatter x1, waiting for transfers between devices: 34.9 us -> 1.53 us  [per_device(): lax.psum_scatter(jnp.dot(act_all, wout_tile, preferred_element_type=jnp.f...]
    reduce_scatter x1, waiting for transfers between devices: 40.9 us -> 10.1 us  [per_device(): lax.psum_scatter(jnp.dot(tok_rows, win_tile, preferred_element_type=jnp.f...]
    reduce_scatter x1, waiting for transfers between devices: 17.5 us -> 34.9 us  [per_device(): lax.psum_scatter(contract_last(dpre_all, win_tile), 'gy', scatter_dimensi...]
    another operation x0 -> x1, other arithmetic: none -> 9.88 us  [per_device(): jnp.stack([w_in] * lax.axis_size('gx'))]
    unnamed x7 -> x11, local copies, waits for them, and re-layouts: 7.41 us -> 16.4 us
  transfers between devices with their start and end apart: 10 -> 10, of which waited for: 10 -> 9; matrix products, arithmetic and copies ran while one was open for 8% -> 11% of each run, Pallas kernels for 0% -> 0%
where the time goes in v1:
time: 663 us; the launch traced here: 662 us
  waiting for transfers between devices  514 us (78%)
  blocking collectives  41.6 us (6%)
  matrix products  41.3 us (6%)
  other arithmetic  24.5 us (4%)
  local copies, waits for them, and re-layouts  16.4 us (2%)
  between operations  15.6 us (2%)
  starting transfers between devices  8.53 us (1%)
    all_to_all x1, waiting for transfers between devices, per_device(): lax.all_to_all(jnp.stack([w_in] * lax.axis_size('gx')), 'gx', 0, 0)  177 us
    reduce_scatter x1, waiting for transfers between devices, per_device(): lax.psum_scatter(win_term.astype(jnp.bfloat16), 'gx', scatter_dimension=1...  111 us
    reduce_scatter x1, waiting for transfers between devices, per_device(): lax.psum_scatter((contract_first(act_all, grad_rows) * block_scale).astyp...  105 us
    reduce_scatter x1, waiting for transfers between devices, per_device(): lax.psum_scatter(contract_last(grad_rows, wout_tile), 'gz', scatter_dimen...  40.7 us
    reduce_scatter x1, waiting for transfers between devices, per_device(): lax.psum_scatter(contract_last(dpre_all, win_tile), 'gy', scatter_dimensi...  34.9 us
    all_gather x1, blocking collectives, per_device(): lax.all_gather(tokens, 'gy', axis=0, tiled=True)  22.1 us
    all_gather x1, blocking collectives, per_device(): lax.all_gather(grad_out, 'gy', axis=0, tiled=True)  19.6 us
    all_gather x1, waiting for transfers between devices, per_device(): act_all = lax.all_gather(act_part, 'gz', axis=0, tiled=True)  18.8 us
  transfers between devices with their start and end apart: 10, of which 9 were waited for; matrix products, arithmetic and copies ran while one was open for 11% of the time, Pallas kernels for 0%

profile of v1, /device:TPU:0, one launch (start us, length us, event | category | flops | bytes accessed | tf_op | source)
XLA Modules:
  0.0 662.0 jit_solution(3224236834754509280)
XLA Ops:
  8.0 0.7 all-gather.6.cloned.1.call-update
  8.7 6.6 copy.18
  15.3 9.9 %pad_maximum_fusion = bf16[2,1536,1536]{1,2,0:T(8,128)(2,1)} fusion(bf16[1,1536,1536]{1,2,0:T(8,128)(2,1)} %bitcast.22), kind=kLoop, calls=%fused_computation.3 | loop fusion | flops 4718592 | bytes 14155776 | tf_op jit(solution)/shard_map/stack | solution.py:33
  25.2 8.0 %all-to-all-start = ((bf16[2,1536,1536]{1,2,0:T(8,128)(2,1)}), bf16[2,1536,1536]{1,2,0:T(8,128)(2,1)}, u32[]{:S(2)}, u32[]{:S(2)}) async-start(bf16[2,1536,1536]{1,2,0:T(8,128)(2,1)} %pad_maximum_fusion), calls=%async_computation | async-start | bytes 18874368 | tf_op jit(solution)/shard_map/all_to_all | solution.py:33
  33.2 0.0 reduce-scatter.19.cloned.1.call-start
  33.3 22.1 %all_gather.15 = bf16[256,1536]{1,0:T(8,128)(2,1)} all-gather(bf16[64,1536]{1,0:T(8,128)(2,1)S(1)} %copy-done.1), channel_id=1, replica_groups=mesh['gx'=2,'gy'=4,'gz'=4] {'gy'}, dimensions={0}, use_global_device_ids=true | all-gather | bytes 983040 | tf_op jit(solution)/shard_map/all_gather | solution.py:28
  55.3 176.8 %all-to-all-done = bf16[2,1536,1536]{1,2,0:T(8,128)(2,1)} async-done(((bf16[2,1536,1536]{1,2,0:T(8,128)(2,1)}), bf16[2,1536,1536]{1,2,0:T(8,128)(2,1)}, u32[]{:S(2)}, u32[]{:S(2)}) %all-to-all-start) | async-done | bytes 9437216 | tf_op jit(solution)/shard_map/all_to_all | solution.py:33
  232.1 5.5 convolution_bitcast_fusion
  237.6 2.4 copy.29
  240.0 0.0 reduce-scatter.21.cloned.1.call-start
  240.0 19.6 %all_gather.18 = bf16[256,1536]{1,0:T(8,128)(2,1)S(1)} all-gather(bf16[64,1536]{1,0:T(8,128)(2,1)S(1)} %copy-done.2), channel_id=1, replica_groups=mesh['gx'=2,'gy'=4,'gz'=4] {'gy'}, dimensions={0}, use_global_device_ids=true | all-gather | bytes 983040 | tf_op jit(solution)/shard_map/all_gather | solution.py:29
  259.6 8.0 %fusion.18 = f32[256,3072]{1,0:T(8,128)} fusion(bf16[256,1536]{1,0:T(8,128)(2,1)S(1)} %all_gather.18, bf16[3072,1536]{1,0:T(8,128)(2,1)} %all-gather.6.cloned.1.call-done), kind=kOutput, calls=%fused_computation.32 | convolution fusion | flops 2415919104 | bytes 13369344
  267.6 0.0 all-gather.4.cloned.1.call-start
  267.6 10.1 %reduce-scatter.19.cloned.1.call-done = f32[64,3072]{1,0:T(8,128)} async-done(((f32[256,3072]{1,0:T(8,128)}), f32[64,3072]{1,0:T(8,128)}) %reduce-scatter.19.cloned.1.call-update) | async-done | bytes 786448 | tf_op jit(solution)/shard_map/reduce_scatter | solution.py:39
  277.8 40.7 %reduce-scatter.21.cloned.1.call-done = f32[64,3072]{1,0:T(8,128)} async-done(((f32[256,3072]{1,0:T(8,128)}), f32[64,3072]{1,0:T(8,128)}) %reduce-scatter.21.cloned.1.call-update) | async-done | bytes 786448 | tf_op jit(solution)/shard_map/reduce_scatter | solution.py:59
  318.5 3.8 fusion.9
  322.4 0.7 all-gather.8.cloned.1.call-update
  323.2 18.8 %all-gather.4.cloned.1.call-done = bf16[256,3072]{1,0:T(8,128)(2,1)} async-done(((bf16[64,3072]{1,0:T(8,128)(2,1)}), bf16[256,3072]{1,0:T(8,128)(2,1)}) %all-gather.4.cloned.1.call-update) | async-done | bytes 1572880 | tf_op jit(solution)/shard_map/all_gather | solution.py:46
  342.0 7.9 %fusion.17 = f32[256,1536]{1,0:T(8,128)} fusion(bf16[256,3072]{1,0:T(8,128)(2,1)} %all-gather.4.cloned.1.call-done, bf16[3072,1536]{1,0:T(8,128)(2,1)} %all-gather.6.cloned.1.call-done), kind=kOutput, calls=%fused_computation.31 | convolution fusion | flops 2415919104 | bytes 12582912 | tf_op jit(solution)/shard_map/dot_general | solution.py:48
  350.0 13.7 %all-gather.8.cloned.1.call-done = bf16[256,3072]{1,0:T(8,128)(2,1)} async-done(((bf16[64,3072]{1,0:T(8,128)(2,1)}), bf16[256,3072]{1,0:T(8,128)(2,1)}) %all-gather.8.cloned.1.call-update) | async-done | bytes 1572880 | tf_op jit(solution)/shard_map/all_gather | solution.py:63
  363.7 8.1 %fusion.19 = f32[256,1536]{1,0:T(8,128)} fusion(bf16[256,3072]{1,0:T(8,128)(2,1)} %all-gather.8.cloned.1.call-done, bf16[1536,3072]{0,1:T(8,128)(2,1)} %bitcast.2), kind=kOutput, calls=%fused_computation.33 | convolution fusion | flops 2415919104 | bytes 12582912 | tf_op jit(solution)/shard_map/dot_general | solution.py:15
  371.8 6.7 %fusion = bf16[1536,3072]{0,1:T(8,128)(2,1)} fusion(bf16[256,3072]{1,0:T(8,128)(2,1)} %all-gather.8.cloned.1.call-done, bf16[256,1536]{1,0:T(8,128)(2,1)S(1)} %copy-done), kind=kOutput, calls=%fused_computation.2 | convolution fusion | flops 2425356288 | bytes 11796480 | tf_op jit(solution)/shard_map/dot_general | solution.py:21
  378.6 0.2 reduce-scatter.17.cloned.1.call-start
  378.8 5.1 multiply_convert_fusion
  384.0 1.5 reduce-scatter.11.cloned.1.call-done
  385.5 1.7 convert_element_type.28
  387.2 34.9 %reduce-scatter.13.cloned.1.call-done = f32[64,1536]{1,0:T(8,128)} async-done(((f32[256,1536]{1,0:T(8,128)}), f32[64,1536]{1,0:T(8,128)}) %reduce-scatter.13.cloned.1.call-update) | async-done | bytes 393232 | tf_op jit(solution)/shard_map/reduce_scatter | solution.py:64
  422.1 1.7 convert_element_type.30
  423.8 110.6 %reduce-scatter.15.cloned.1.call-done = bf16[1536,1536]{0,1:T(8,128)(2,1)} async-done(((bf16[1536,3072]{0,1:T(8,128)(2,1)}), bf16[1536,1536]{0,1:T(8,128)(2,1)}) %reduce-scatter.15.cloned.1.call-update) | async-done | bytes 4718608 | tf_op jit(solution)/shard_map/reduce_scatter | solution.py:68
  534.4 7.4 %copy.27 = f32[1536,1536]{1,0:T(8,128)} copy(bf16[1536,1536]{0,1:T(8,128)(2,1)} %reduce-scatter.15.cloned.1.call-done) | data formatting | bytes 14155776
  541.8 105.4 %reduce-scatter.17.cloned.1.call-done = bf16[1536,1536]{1,0:T(8,128)(2,1)} async-done(((bf16[3072,1536]{1,0:T(8,128)(2,1)}), bf16[1536,1536]{1,0:T(8,128)(2,1)}) %reduce-scatter.17.cloned.1.call-update) | async-done | bytes 4718608 | tf_op jit(solution)/shard_map/reduce_scatter | solution.py:53
  647.2 7.4 %convert_element_type.35 = f32[1536,1536]{1,0:T(8,128)} convert(bf16[1536,1536]{1,0:T(8,128)(2,1)} %reduce-scatter.17.cloned.1.call-done) | non-fusion elementwise | flops 2359296 | bytes 14155776 | tf_op jit(solution)/shard_map/convert_element_type | solution.py:58
  (21 shorter events, 0.3 us)
Async XLA Ops:
  8.0 251.6 %all-gather.6.cloned.1.call-start = ((), (), s32[]{:S(2)}) async-start(), calls=%async_computation.8 | async-start | bytes 14155776 | tf_op jit(solution)/shard_map/all_gather | solution.py:35
  25.2 8.0 %copy-start.1 = (bf16[64,1536]{1,0:T(8,128)(2,1)S(1)}, bf16[64,1536]{1,0:T(8,128)(2,1)}, u32[]{:S(2)}) copy-start(bf16[64,1536]{1,0:T(8,128)(2,1)} %param.4) | copy-start | bytes 589828
  25.2 206.8 %all-to-all-start = ((bf16[2,1536,1536]{1,2,0:T(8,128)(2,1)}), bf16[2,1536,1536]{1,2,0:T(8,128)(2,1)}, u32[]{:S(2)}, u32[]{:S(2)}) async-start(bf16[2,1536,1536]{1,2,0:T(8,128)(2,1)} %pad_maximum_fusion), calls=%async_computation | async-start | bytes 18874368 | tf_op jit(solution)/shard_map/all_to_all | solution.py:33
  33.2 244.6 %reduce-scatter.19.cloned.1.call-start = ((), (), s32[]{:S(2)}) async-start(), calls=%async_computation.14 | async-start | bytes 3932160 | tf_op jit(solution)/shard_map/reduce_scatter | solution.py:39
  232.1 7.9 %copy-start.2 = (bf16[64,1536]{1,0:T(8,128)(2,1)S(1)}, bf16[64,1536]{1,0:T(8,128)(2,1)}, u32[]{:S(2)}) copy-start(bf16[64,1536]{1,0:T(8,128)(2,1)} %param.5) | copy-start | bytes 589828
  240.0 78.6 %reduce-scatter.21.cloned.1.call-start = ((), (), s32[]{:S(2)}) async-start(), calls=%async_computation.15 | async-start | bytes 3932160 | tf_op jit(solution)/shard_map/reduce_scatter | solution.py:59
  267.6 74.4 %all-gather.4.cloned.1.call-start = ((), (), s32[]{:S(2)}) async-start(), calls=%async_computation.7 | async-start | bytes 1966080 | tf_op jit(solution)/shard_map/all_gather | solution.py:46
  322.4 41.3 %all-gather.8.cloned.1.call-start = ((), (), s32[]{:S(2)}) async-start(), calls=%async_computation.10 | async-start | bytes 1966080 | tf_op jit(solution)/shard_map/all_gather | solution.py:63
  323.1 62.4 %reduce-scatter.11.cloned.1.call-start = ((), (), s32[]{:S(2)}) async-start(), calls=%async_computation.9 | async-start | bytes 1966080 | tf_op jit(solution)/shard_map/reduce_scatter | solution.py:47
  349.9 21.9 %copy-start = (bf16[256,1536]{1,0:T(8,128)(2,1)S(1)}, bf16[256,1536]{1,0:T(8,128)(2,1)}, u32[]{:S(2)}) copy-start(bf16[256,1536]{1,0:T(8,128)(2,1)} %all_gather.15) | copy-start | bytes 2359300
  349.9 72.2 %reduce-scatter.13.cloned.1.call-start = ((), (), s32[]{:S(2)}) async-start(), calls=%async_computation.11 | async-start | bytes 1966080 | tf_op jit(solution)/shard_map/reduce_scatter | solution.py:64
  371.8 7.1 %copy-start.3 = (bf16[256,3072]{1,0:T(8,128)(2,1)S(1)}, bf16[256,3072]{1,0:T(8,128)(2,1)}, u32[]{:S(2)}) copy-start(bf16[256,3072]{1,0:T(8,128)(2,1)} %all-gather.4.cloned.1.call-done) | copy-start | bytes 4718596
  371.8 162.6 %reduce-scatter.15.cloned.1.call-start = ((), (), s32[]{:S(2)}) async-start(), calls=%async_computation.12 | async-start | bytes 14155776 | tf_op jit(solution)/shard_map/reduce_scatter | solution.py:68
  378.6 268.6 %reduce-scatter.17.cloned.1.call-start = ((), (), s32[]{:S(2)}) async-start(), calls=%async_computation.13 | async-start | bytes 14155776 | tf_op jit(solution)/shard_map/reduce_scatter | solution.py:53
Sparse Core Ops, SparseCore 0:
  10.4 214.0 all-gather.5
  350.0 35.4 reduce-scatter.10
  387.8 34.2 reduce-scatter.12
  424.9 109.4 reduce-scatter.14
  536.5 110.6 reduce-scatter.16
Sparse Core Ops, SparseCore 1:
  240.0 37.7 reduce-scatter.18
  280.8 37.7 reduce-scatter.20
  322.5 19.5 all-gather.3
  344.2 19.5 all-gather.7
